TPU v7x, 64 devices: a 2x2x8 block of a 4x4x8 slice. The times are simulated.
64 devices in a mesh: dp: 4 (over x, y), tp: 16 (over z, core).
Axes of the slice: x: 2, y: 2, z: 8, core: 2. Of those that a mesh axis runs over, the one named last changes fastest.
The devices are a block of a 4x4x8 slice.
Arguments:
- token_ids: int32 [4, 2048], P('dp'), parts along dimension 0
- word_table: bfloat16 [50432, 6144], P('tp')
- pos_table: bfloat16 [2048, 6144], replicated
- ln_gain: float32 [6144], replicated
- ln_bias: float32 [6144], replicated
- w_qkv: bfloat16 [6144, 3, 64, 96], P(None, None, 'tp')
- b_qkv: float32 [3, 64, 96], P(None, 'tp')
- w_out: bfloat16 [64, 96, 6144], P('tp')
- b_out: float32 [6144], replicated
Outputs:
- output 1: bfloat16 [4, 2048, 6144], P('dp', 'tp'), parts along dimension 0
- output 2: bfloat16 [4, 2048, 6144], P('dp', 'tp'), parts along dimension 0
There are 4 independent parts. A program takes and returns all parts, laid end to end along the dimension named above; an argument that names none is the same for every part.
All inputs are finite; a program needn't handle non-finite values.
Results may differ from a plain program's by a relative error of at most 0.00753435.
Values are sent between devices in bfloat16 or wider.
A program may use at most 768 MiB of HBM per device.

v0:
```python
import jax
import jax.numpy as jnp
from jax import lax
from jax.sharding import PartitionSpec as P

LN_EPS = 1e-5


def layer_norm(values, gain, bias):
    feat_mean = jnp.mean(values, axis=-1, keepdims=True)
    centered = values - feat_mean
    feat_variance = jnp.mean(centered * centered, axis=-1, keepdims=True)
    return centered * lax.rsqrt(feat_variance + LN_EPS) * gain + bias


def head_outputs(normed, w_qkv, b_qkv, w_out):
    seq_len = normed.shape[1]
    head_dim = w_qkv.shape[-1]
    projected = jnp.einsum("bsd,dche->cbhse", normed, w_qkv, preferred_element_type=jnp.float32)
    projected = (projected + b_qkv[:, None, :, None, :]).astype(jnp.bfloat16)
    attn_scores = jnp.einsum("bhqe,bhke->bhqk", projected[0], projected[1], preferred_element_type=jnp.float32) * head_dim ** -0.5
    causal_mask = lax.broadcasted_iota(jnp.int32, (seq_len, seq_len), 0) >= lax.broadcasted_iota(jnp.int32, (seq_len, seq_len), 1)
    attn_scores = jnp.where(causal_mask, attn_scores, -jnp.inf)
    attn_probs = jax.nn.softmax(attn_scores, axis=-1).astype(jnp.bfloat16)
    context = jnp.einsum("bhqk,bhke->bhqe", attn_probs, projected[2], preferred_element_type=jnp.float32).astype(jnp.bfloat16)
    return jnp.einsum("cirf,ife->cre", context, w_out, preferred_element_type=jnp.float32)


def solution(mesh):
    tp_size = mesh.shape["tp"]

    def local_step(token_ids, word_shard, pos_table, ln_gain, ln_bias, w_qkv, b_qkv, w_out, b_out):
        shard_rows = word_shard.shape[0]
        block_len = token_ids.shape[1] // tp_size
        tp_index = lax.axis_index("tp")
        local_ids = token_ids - tp_index * shard_rows
        in_shard = (local_ids >= 0) & (local_ids < shard_rows)
        table_rows = jnp.take(word_shard, local_ids, axis=0, mode="clip")
        partial_rows = jnp.where(in_shard[:, :, None], table_rows, jnp.zeros((), jnp.bfloat16))
        block_rows = lax.psum_scatter(partial_rows, "tp", scatter_dimension=1, tiled=True)
        pos_block = lax.dynamic_slice_in_dim(pos_table, tp_index * block_len, block_len, axis=0)
        embed = (block_rows.astype(jnp.float32) + pos_block.astype(jnp.float32)[None]).astype(jnp.bfloat16)
        normed_block = layer_norm(embed.astype(jnp.float32), ln_gain, ln_bias).astype(jnp.bfloat16)
        normed = lax.all_gather(normed_block, "tp", axis=1, tiled=True)
        partial_out = head_outputs(normed, w_qkv, b_qkv, w_out)
        out_block = lax.psum_scatter(partial_out, "tp", scatter_dimension=1, tiled=True)
        resid_out = (embed.astype(jnp.float32) + out_block + b_out).astype(jnp.bfloat16)
        return resid_out, embed

    in_specs = (P("dp", None), P("tp", None), P(None, None), P(None), P(None), P(None, None, "tp", None), P(None, "tp", None), P("tp", None, None), P(None))
    out_specs = (P("dp", "tp", None), P("dp", "tp", None))
    return jax.shard_map(local_step, mesh=mesh, in_specs=in_specs, out_specs=out_specs, check_vma=False)
```

profile of v0, /device:TPU:21, one launch (start us, length us, event | category | flops | bytes accessed | tf_op | source)
XLA Modules:
  0.0 909.4 jit_solution(3289911139268972556)
XLA Ops:
  7.2 0.1 reduce-scatter.3.cloned.1.call-start
  7.2 0.7 and_reduce_fusion
  8.0 139.1 %gather_fusion = bf16[2048,6144]{1,0:T(8,128)(2,1)} fusion(bf16[3152,6144]{1,0:T(8,128)(2,1)} %param.10, s32[2048]{0:T(1024)S(1)} %broadcast_clamp_fusion), kind=kCustom, calls=%fused_computation | custom fusion | bytes 50339840 | tf_op jit(solution)/shard_map/jit(_take)/gather | solution.py:38
  147.1 21.6 %bitcast_select_fusion = bf16[1,2048,6144]{2,1,0:T(8,128)(2,1)} fusion(bf16[2048,6144]{1,0:T(8,128)(2,1)} %gather_fusion, pred[2048]{0:T(1024)(128)(4,1)S(1)} %get-tuple-element.4), kind=kLoop, calls=%fused_computation.13 | loop fusion | flops 12582912 | bytes 50333696 | tf_op jit(solution)/shard_map/jit(_where)/select_n | solution.py:39
  168.7 0.1 reduce-scatter.3.cloned.1.call-update
  168.8 0.0 copy-start.2
  168.8 0.0 copy-start.3
  168.8 0.1 all-gather.2.cloned.1.call-start
  168.9 212.4 %reduce-scatter.3.cloned.1.call-done = bf16[1,128,6144]{2,1,0:T(8,128)(2,1)} async-done(((bf16[1,2048,6144]{2,1,0:T(8,128)(2,1)}), bf16[1,128,6144]{2,1,0:T(8,128)(2,1)}) %reduce-scatter.3.cloned.1.call-update) | async-done | bytes 1572880 | tf_op jit(solution)/shard_map/reduce_scatter | solution.py:40
  381.3 2.6 convert_reduce_fusion
  383.9 0.0 copy-start
  383.9 0.6 fusion.13
  384.5 0.5 copy-done
  385.1 0.0 copy-done.2
  385.1 0.0 copy-done.3
  385.1 1.8 fusion.16
  386.9 0.1 all-gather.2.cloned.1.call-update
  386.9 0.1 reduce-scatter.5.cloned.1.call-start
  387.0 4.1 iota_compare_fusion
  391.1 127.1 %all-gather.2.cloned.1.call-done = bf16[1,2048,6144]{2,1,0:T(8,128)(2,1)} async-done(((bf16[1,128,6144]{2,1,0:T(8,128)(2,1)}), bf16[1,2048,6144]{2,1,0:T(8,128)(2,1)}) %all-gather.2.cloned.1.call-update) | async-done | bytes 25165840 | tf_op jit(solution)/shard_map/all_gather | solution.py:44
  518.2 0.0 copy-start.5
  518.2 35.0 %fusion.6 = f32[2048,1152]{0,1:S(1)} fusion(bf16[6144,1152]{0,1:T(8,128)(2,1)} %bitcast.57, bf16[1,2048,6144]{2,1,0:T(8,128)(2,1)} %all-gather.2.cloned.1.call-done), kind=kOutput, calls=%fused_computation.11 | convolution fusion | flops 28991029248 | bytes 48758784
  553.2 0.0 copy-done.5
  553.2 2.7 fusion.10
  555.9 35.0 %fusion.25 = (f32[4,2048]{1,0:T(4,128)S(1)}, f32[4,2048,2048]{1,2,0:T(8,128)}) fusion(pred[2048,2048]{0,1:T(8,128)(4,1)} %iota_compare_fusion, bf16[3,1,4,2048,96]{3,4,2,0,1:T(8,128)(2,1)} %fusion.10), kind=kOutput, calls=%fused_computation.43 | convolution fusion | flops 3288336384 | bytes 74481664 | tf_op jit(solution)/shard_map/sub | solution.py:24
  590.9 22.3 %fusion.20.clone.4 = bf16[4,2048,96]{1,2,0:T(8,128)(2,1)S(1)} fusion(f32[4,2048,2048]{1,2,0:T(8,128)} %get-tuple-element.7, f32[4,2048]{1,0:T(4,128)S(1)} %get-tuple-element.6, bf16[3,1,4,2048,96]{3,4,2,0,1:T(8,128)(2,1)} %fusion.10), kind=kOutput, calls=%fused_computation.31.clone.clone.clone.1 | convolution fusion | flops 3255566336 | bytes 70287360 | tf_op jit(solution)/shard_map/bhqk,bhke->bhqe/dot_general | solution.py:25
  613.3 22.3 %convolution_bitcast_fusion = f32[1,2048,6144]{2,1,0:T(8,128)} fusion(bf16[4,96,6144]{2,1,0:T(8,128)(2,1)} %param.16, bf16[4,2048,96]{1,2,0:T(8,128)(2,1)S(1)} %fusion.20.clone.4), kind=kOutput, calls=%fused_computation.10 | convolution fusion | flops 9663676416 | bytes 56623104 | tf_op jit(solution)/shard_map/cirf,ife->cre/dot_general | solution.py:26
  635.6 0.0 copy-start.1
  635.6 0.0 copy-start.4
  635.6 0.1 reduce-scatter.5.cloned.1.call-update
  635.7 263.8 %reduce-scatter.5.cloned.1.call-done = f32[1,128,6144]{2,1,0:T(8,128)} async-done(((f32[1,2048,6144]{2,1,0:T(8,128)}), f32[1,128,6144]{2,1,0:T(8,128)}) %reduce-scatter.5.cloned.1.call-update) | async-done | bytes 3145744 | tf_op jit(solution)/shard_map/reduce_scatter | solution.py:46
  899.4 0.0 copy-done.1
  899.4 0.0 copy-done.4
  899.4 3.4 fusion.18
  (3 shorter events, 0.0 us)
Async XLA Ops:
  7.2 374.2 %reduce-scatter.3.cloned.1.call-start = ((), (), s32[]{:S(2)}) async-start(), calls=%async_computation.2 | async-start | bytes 26738688 | tf_op jit(solution)/shard_map/reduce_scatter | solution.py:40
  168.8 216.2 %copy-start.2 = (f32[6144]{0:T(1024)S(1)}, f32[6144]{0:T(1024)}, u32[]{:S(2)}) copy-start(f32[6144]{0:T(1024)} %param.13) | copy-start | bytes 73732
  168.8 216.2 %copy-start.3 = (f32[6144]{0:T(1024)S(1)}, f32[6144]{0:T(1024)}, u32[]{:S(2)}) copy-start(f32[6144]{0:T(1024)} %param.12) | copy-start | bytes 73732
  168.8 349.4 %all-gather.2.cloned.1.call-start = ((), (), s32[]{:S(2)}) async-start(), calls=%async_computation.3 | async-start | bytes 26738688 | tf_op jit(solution)/shard_map/all_gather | solution.py:44
  383.9 1.1 copy-start
  386.9 512.5 %reduce-scatter.5.cloned.1.call-start = ((), (), s32[]{:S(2)}) async-start(), calls=%async_computation.4 | async-start | bytes 53477376 | tf_op jit(solution)/shard_map/reduce_scatter | solution.py:46
  518.2 35.0 %copy-start.5 = (f32[3,4,96]{2,1,0:T(4,128)S(1)}, f32[3,4,96]{2,1,0:T(4,128)}, u32[]{:S(2)}) copy-start(f32[3,4,96]{2,1,0:T(4,128)} %param.15) | copy-start | bytes 13828
  635.6 263.9 %copy-start.1 = (bf16[1,128,6144]{2,1,0:T(8,128)(2,1)S(1)}, bf16[1,128,6144]{2,1,0:T(8,128)(2,1)}, u32[]{:S(2)}) copy-start(bf16[1,128,6144]{2,1,0:T(8,128)(2,1)} %copy-done) | copy-start | bytes 4718596
  635.6 263.9 %copy-start.4 = (f32[6144]{0:T(1024)S(1)}, f32[6144]{0:T(1024)}, u32[]{:S(2)}) copy-start(f32[6144]{0:T(1024)} %param.17) | copy-start | bytes 73732
Sparse Core Ops, SparseCore 0:
  168.9 212.3 reduce-scatter.2
  387.1 131.1 all-gather.1
  635.8 263.6 reduce-scatter.4
where the time goes:
time: 912 us; the launch traced here: 909 us
  waiting for transfers between devices  603 us (66%)
  local copies, waits for them, and re-layouts  140 us (15%)
  matrix products  115 us (13%)
  other arithmetic  37.6 us (4%)
  between operations  13.9 us (2%)
    reduce_scatter x1, waiting for transfers between devices, local_step(): lax.psum_scatter(partial_out, 'tp', scatter_dimension=1, tiled=True)  264 us
    reduce_scatter x1, waiting for transfers between devices, local_step(): lax.psum_scatter(partial_rows, 'tp', scatter_dimension=1, tiled=True)  212 us
    gather x1, local copies, waits for them, and re-layouts, local_step(): table_rows = jnp.take(word_shard, local_ids, axis=0, mode='clip')  139 us
    all_gather x1, waiting for transfers between devices, local_step(): normed = lax.all_gather(normed_block, 'tp', axis=1, tiled=True)  127 us
    sub x1, matrix products, head_outputs(): attn_probs = jax.nn.softmax(attn_scores, axis=-1).astype(jnp.bfloat16)  35 us
    unnamed x1, matrix products  35 us
    dot_general x1, matrix products, head_outputs(): jnp.einsum('bhqk,bhke->bhqe', attn_probs, projected[2], preferred_element...  22.3 us
    dot_general x1, matrix products, head_outputs(): jnp.einsum('cirf,ife->cre', context, w_out, preferred_element_type=jnp.fl...  22.3 us
  transfers between devices with their start and end apart: 3, of which 3 were waited for; matrix products, arithmetic and copies ran while one was open for 0% of the time, Pallas kernels for 0%

commit v1 on v0

v1 whole, which is shorter than its diff:
```python
import functools

import jax
import jax.numpy as jnp
from jax import lax
from jax.experimental import pallas as pl
from jax.experimental.pallas import tpu as pltpu
from jax.sharding import PartitionSpec as P

LN_EPS = 1e-5
MESH = pl.DeviceIdType.MESH
BF16 = jnp.bfloat16
F32 = jnp.float32
VMEM_LIMIT = 67043328


def layer_norm(values, gain, bias):
    feat_mean = jnp.mean(values, axis=-1, keepdims=True)
    centered = values - feat_mean
    feat_variance = jnp.mean(centered * centered, axis=-1, keepdims=True)
    return centered * lax.rsqrt(feat_variance + LN_EPS) * gain + bias


ROWS = 16
FETCHES = 16
NONE = -(2**30)


def gather_kernel(block_len, shard_rows, ids_ref, column_ref, table_ref, out_ref, found, count, stamp, fetched, sems):
    j = pl.program_id(0)
    n_blocks = pl.num_programs(0)
    n_groups = shard_rows // ROWS

    def scan(block):
        base = lax.rem(block, 2) * (2 * block_len)

        def one(q, total):
            local_id = ids_ref[block * block_len + q]
            mine = (local_id >= 0) & (local_id < shard_rows)
            group = jnp.where(mine, lax.div(local_id, ROWS), n_groups)
            fresh = mine & (stamp[group] != block)
            stamp[group] = block
            found[base + total] = group
            return total + jnp.where(fresh, 1, 0)

        count[lax.rem(block, 2)] = lax.fori_loop(0, block_len, one, 0, unroll=8)

    def copy_of(block, chunk, k, slot):
        group = found[lax.rem(block, 2) * (2 * block_len) + chunk * FETCHES + k]
        return pltpu.make_async_copy(
            table_ref.at[pl.ds(pl.multiple_of(group * ROWS, ROWS), ROWS), :],
            fetched.at[slot, pl.ds(pl.multiple_of(k * ROWS, ROWS), ROWS), :],
            sems.at[slot, k],
        )

    def in_chunk(block, chunk):
        return jnp.minimum(count[lax.rem(block, 2)] - chunk * FETCHES, FETCHES)

    def start(block, chunk, slot):
        def one(k, carry):
            copy_of(block, chunk, k, slot).start()
            return carry

        lax.fori_loop(0, in_chunk(block, chunk), one, 0)

    def wait(block, chunk, slot):
        def one(k, carry):
            copy_of(block, chunk, k, slot).wait()
            return carry

        lax.fori_loop(0, in_chunk(block, chunk), one, 0)

    def selector(block, chunk):
        columns = lax.broadcasted_iota(jnp.int32, (1, FETCHES * ROWS), 1)
        base = lax.rem(block, 2) * (2 * block_len) + chunk * FETCHES
        held = in_chunk(block, chunk)
        first = jnp.full((1, FETCHES * ROWS), NONE, jnp.int32)
        for k in range(FETCHES):
            first = jnp.where(lax.div(columns, ROWS) == k, jnp.where(k < held, found[base + k] * ROWS, NONE), first)
        return jnp.where(column_ref[...] == first + lax.rem(columns, ROWS), 1.0, 0.0).astype(BF16)

    @pl.when(j == 0)
    def _():
        fetched[...] = jnp.zeros_like(fetched)

        def clear(g, carry):
            stamp[g] = -1
            return carry

        lax.fori_loop(0, n_groups + 1, clear, 0)
        scan(0)
        start(0, 0, 0)

    @pl.when(j + 1 < n_blocks)
    def _():
        scan(j + 1)
        start(j + 1, 0, lax.rem(j + 1, 2))

    slot = lax.rem(j, 2)
    wait(j, 0, slot)
    out_ref[...] = jnp.dot(selector(j, 0), fetched[slot], preferred_element_type=F32).astype(BF16)

    def more(chunk, carry):
        start(j, chunk, slot)
        wait(j, chunk, slot)
        out_ref[...] += jnp.dot(selector(j, chunk), fetched[slot], preferred_element_type=F32).astype(BF16)
        return carry

    lax.fori_loop(1, lax.div(count[slot] + (FETCHES - 1), FETCHES), more, 0)


def gather_rows(local_ids, table, block_len):
    (n_ids,), (shard_rows, width) = local_ids.shape, table.shape
    return pl.pallas_call(
        functools.partial(gather_kernel, block_len, shard_rows),
        grid=(n_ids // block_len,),
        out_shape=jax.ShapeDtypeStruct((n_ids, width), BF16),
        in_specs=[
            pl.BlockSpec(memory_space=pltpu.SMEM),
            pl.BlockSpec((block_len, 1), lambda j: (j, 0)),
            pl.BlockSpec(memory_space=pl.ANY),
        ],
        out_specs=pl.BlockSpec((block_len, width), lambda j: (j, 0)),
        scratch_shapes=[
            pltpu.SMEM((4 * block_len,), jnp.int32),
            pltpu.SMEM((2,), jnp.int32),
            pltpu.SMEM((shard_rows // ROWS + 1,), jnp.int32),
            pltpu.VMEM((2, FETCHES * ROWS, width), BF16),
            pltpu.SemaphoreType.DMA((2, FETCHES)),
        ],
        compiler_params=pltpu.CompilerParams(vmem_limit_bytes=40 * 2**20),
        name="gather_rows",
    )(local_ids, local_ids.reshape(n_ids, 1), table)


class Ring:
    def __init__(self, n):
        self.chips = n // 2
        self.me = lax.axis_index("tp")
        self.odd = lax.rem(self.me, 2)
        self.chip = lax.div(self.me, 2)
        self.way = 2 * self.odd - 1
        self.near = self.me - self.way
        self.far = lax.rem(self.me + self.way + n, n)

    def near_block(self, k):
        return 2 * lax.rem(self.chip - self.way * k + 2 * self.chips, self.chips) + self.odd

    def far_block(self, k):
        return 2 * lax.rem(self.chip + self.way * k + 2 * self.chips, self.chips) + 1 - self.odd

    def barrier(self):
        sem = pltpu.get_barrier_semaphore()
        for device in (self.near, self.far):
            pl.semaphore_signal(sem, inc=1, device_id={"tp": device}, device_id_type=MESH)
        pl.semaphore_wait(sem, 2)


def remote(src, dst, send_sem, recv_sem, device):
    return pltpu.make_async_remote_copy(
        src_ref=src, dst_ref=dst, send_sem=send_sem, recv_sem=recv_sem, device_id={"tp": device}, device_id_type=MESH
    )


def ring_sum_kernel(n, part_ref, out_ref, own_n, own_f, buf_n, buf_f, own_sem, send_f, send_n, recv_f, recv_n):
    ring = Ring(n)

    def load_n(t):
        return pltpu.make_async_copy(part_ref.at[ring.near_block(lax.div(t, 2) + 1), lax.rem(t, 2)], own_n.at[t], own_sem.at[0, t])

    def load_f(t):
        return pltpu.make_async_copy(part_ref.at[ring.far_block(lax.div(t, 2) + 1), lax.rem(t, 2)], own_f.at[t], own_sem.at[1, t])

    def start_loads(t, carry):
        load_f(t).start()
        load_n(t).start()
        return carry

    lax.fori_loop(0, n, start_loads, 0)
    ring.barrier()

    def to_far(src, t):
        return remote(src, buf_f.at[t], send_f.at[t], recv_f.at[t], ring.far)

    def to_near(src, t):
        return remote(src, buf_n.at[t], send_n.at[t], recv_n.at[t], ring.near)

    def pass_far_on(t):
        to_far(buf_f.at[t], t).wait_recv()
        load_f(t + 2).wait()
        buf_f[t] = buf_f[t] + own_f[t + 2]
        to_near(buf_f.at[t], t + 2).start()

    def take_near(t):
        to_near(buf_n.at[t], t).wait_recv()
        load_n(t).wait()

    def pass_near_on(t):
        take_near(t)
        buf_n[t] = buf_n[t] + own_n[t]
        to_far(buf_n.at[t], t).start()

    def finish_near(t):
        take_near(t)
        out_ref[t % 2] = buf_n[t] + own_n[t]

    for t in range(2):
        load_f(t).wait()
        to_near(own_f.at[t], t).start()
    for t in range(2):
        pass_near_on(t)

    def step(t, carry):
        pass_far_on(t)
        pass_near_on(t + 2)
        return carry

    lax.fori_loop(0, n - 4, step, 0)
    for t in (n - 4, n - 3):
        pass_far_on(t)
        finish_near(t + 2)

    def finish(t, carry):
        to_near(own_f.at[t], t).wait_send()
        return carry

    lax.fori_loop(0, n, finish, 0)

    def finish_far(t, carry):
        to_far(buf_n.at[t], t).wait_send()
        return carry

    lax.fori_loop(0, n - 2, finish_far, 0)


def ring_sum(partial_rows, n):
    _, _, half, width = partial_rows.shape
    dma = pltpu.SemaphoreType.DMA
    return pl.pallas_call(
        functools.partial(ring_sum_kernel, n),
        out_shape=jax.ShapeDtypeStruct((2, half, width), BF16),
        in_specs=[pl.BlockSpec(memory_space=pl.ANY)],
        out_specs=pl.BlockSpec(memory_space=pltpu.VMEM),
        scratch_shapes=[
            pltpu.VMEM((n, half, width), BF16),
            pltpu.VMEM((n, half, width), BF16),
            pltpu.VMEM((n, half, width), BF16),
            pltpu.VMEM((n - 2, half, width), BF16),
            dma((2, n)), dma((n - 2,)), dma((n,)), dma((n - 2,)), dma((n,)),
        ],
        compiler_params=pltpu.CompilerParams(collective_id=1, has_side_effects=True, vmem_limit_bytes=VMEM_LIMIT),
        name="ring_sum",
    )(partial_rows)


def ring_qkv_kernel(n, own_ref, w_hbm, bias_ref, out_ref, w_ref, buf_n, buf_f, w_sem, send_f, send_n, recv_f, recv_n):
    ring = Ring(n)
    half, width = own_ref.shape[1:]
    n_parts, part_width = w_ref.shape[:2]
    load_w = pltpu.make_async_copy(w_hbm, w_ref, w_sem.at[0])
    load_w.start()
    ring.barrier()

    def to_far(src, t):
        return remote(src, buf_f.at[t], send_f.at[t], recv_f.at[t], ring.far)

    def to_near(src, t):
        return remote(src, buf_n.at[t], send_n.at[t], recv_n.at[t], ring.near)

    def multiply(rows, block, low, high):
        def one(c, carry):
            product = lax.dot_general(
                rows[...].reshape(2 * half, width), w_ref[c], (((1,), (1,)), ((), ())), preferred_element_type=F32
            )
            product = (product + bias_ref[c]).astype(BF16)
            out_ref[c, block, :, :, :part_width] = product.reshape(2, half, part_width)
            return carry

        lax.fori_loop(low, high, one, 0)

    for t in range(2):
        to_far(own_ref.at[t], t).start()
    for t in range(2):
        to_near(own_ref.at[t], t).start()
    out_ref[...] = jnp.zeros_like(out_ref)
    load_w.wait()
    multiply(own_ref, ring.me, 0, n_parts)
    for t in range(2):
        to_near(buf_n.at[t], t).wait_recv()
    mid = n_parts // 2

    def step(k, carry):
        near_owner = jnp.where(k == 0, ring.near, ring.near_block(k))
        for h in range(2):
            t = 2 * k + h
            to_far(buf_f.at[t], t).wait_recv()
            to_near(buf_f.at[t], t + 2).start()
            if h == 0:
                multiply(buf_n.at[pl.ds(2 * k, 2)], near_owner, 0, mid)
            else:
                multiply(buf_f.at[pl.ds(2 * k, 2)], ring.far_block(k + 1), 0, mid)
            to_near(buf_n.at[t + 2], t + 2).wait_recv()

            @pl.when(t + 2 < n - 2)
            def _():
                to_far(buf_n.at[t + 2], t + 2).start()

            if h == 0:
                multiply(buf_n.at[pl.ds(2 * k, 2)], near_owner, mid, n_parts)
            else:
                multiply(buf_f.at[pl.ds(2 * k, 2)], ring.far_block(k + 1), mid, n_parts)
        return carry

    lax.fori_loop(0, n // 2 - 1, step, 0)
    multiply(buf_n.at[pl.ds(n - 2, 2)], ring.near_block(n // 2 - 1), 0, n_parts)

    def finish(t, carry):
        to_near(own_ref.at[0], t).wait_send()
        return carry

    lax.fori_loop(0, n, finish, 0)

    def finish_far(t, carry):
        to_far(own_ref.at[0], t).wait_send()
        return carry

    lax.fori_loop(0, n - 2, finish_far, 0)


def ring_qkv(normed, w, bias, n):
    _, half, width = normed.shape
    dma = pltpu.SemaphoreType.DMA
    vmem = pl.BlockSpec(memory_space=pltpu.VMEM)
    return pl.pallas_call(
        functools.partial(ring_qkv_kernel, n),
        out_shape=jax.ShapeDtypeStruct((w.shape[0], n, 2, half, 128), BF16),
        in_specs=[vmem, pl.BlockSpec(memory_space=pl.ANY), vmem],
        out_specs=vmem,
        scratch_shapes=[
            pltpu.VMEM(w.shape, BF16),
            pltpu.VMEM((n, half, width), BF16),
            pltpu.VMEM((n - 2, half, width), BF16),
            dma((1,)), dma((n - 2,)), dma((n,)), dma((n - 2,)), dma((n,)),
        ],
        compiler_params=pltpu.CompilerParams(collective_id=2, has_side_effects=True, vmem_limit_bytes=VMEM_LIMIT),
        name="ring_qkv",
    )(normed, w, bias)


def ring_out_kernel(n, slots, qkv_ref, w_ref, embed_ref, bias_ref, out_ref, init_f, add_n, add_f, buf_n, buf_f,
                    send_f, send_n, recv_f, recv_n, free_f, free_n):
    ring = Ring(n)
    heads, head_dim, width = w_ref.shape
    half = embed_ref.shape[1]
    seq_len = qkv_ref.shape[1]
    chunk = width // 4
    scale = head_dim ** -0.5

    def term(block, which, dst):
        first = pl.multiple_of((block * 2 + which) * half, half)
        visible = lax.broadcasted_iota(jnp.int32, (half, seq_len), 1) <= first + lax.broadcasted_iota(jnp.int32, (half, seq_len), 0)
        contexts = []
        for h in range(heads):
            query = qkv_ref[h, pl.ds(first, half), :]
            scores = lax.dot_general(query, qkv_ref[heads + h], (((1,), (1,)), ((), ())), preferred_element_type=F32) * scale
            scores = jnp.where(visible, scores, -jnp.inf)
            scores = jnp.exp(scores - jnp.max(scores, axis=-1, keepdims=True))
            probs = (scores / jnp.sum(scores, axis=-1, keepdims=True)).astype(BF16)
            context = jnp.dot(probs, qkv_ref[2 * heads + h], preferred_element_type=F32).astype(BF16)
            contexts.append(context[:, :head_dim])
        for c in range(width // chunk):
            columns = slice(c * chunk, (c + 1) * chunk)
            total = jnp.dot(contexts[0], w_ref[0, :, columns], preferred_element_type=F32)
            for h in range(1, heads):
                total += jnp.dot(contexts[h], w_ref[h, :, columns], preferred_element_type=F32)
            dst[:, columns] = total

    def near_term(t, dst):
        term(ring.near_block(lax.div(t, 2) + 1), lax.rem(t, 2), dst)

    def far_term(t, dst):
        term(ring.far_block(lax.div(t, 2) + 1), lax.rem(t, 2), dst)

    def to_far(src, t):
        return remote(src, buf_f.at[lax.rem(t, slots)], send_f.at[t], recv_f.at[t], ring.far)

    def to_near(src, t):
        return remote(src, buf_n.at[lax.rem(t, slots)], send_n.at[t], recv_n.at[t], ring.near)

    def pass_far_on(t):
        slot = lax.rem(t, slots)
        to_far(buf_f.at[slot], t).wait_recv()
        buf_f[slot] = buf_f[slot] + add_f[...]

        @pl.when(t + 2 >= slots)
        def _():
            pl.semaphore_wait(free_n, 1)

        to_near(buf_f.at[slot], t + 2).start()

    def pass_near_on(t):
        slot = lax.rem(t, slots)
        to_near(buf_n.at[slot], t).wait_recv()
        buf_n[slot] = buf_n[slot] + add_n[...]

        @pl.when(t >= slots)
        def _():
            pl.semaphore_wait(free_f, 1)

        to_far(buf_n.at[slot], t).start()

    def finish_near(t):
        slot = t % slots
        to_near(buf_n.at[slot], t).wait_recv()
        out_ref[t % 2] = (embed_ref[t % 2].astype(F32) + (buf_n[slot] + add_n[...]) + bias_ref[...]).astype(BF16)

    ring.barrier()

    def begin(t, carry):
        far_term(t, init_f.at[t])
        to_near(init_f.at[t], t).start()
        near_term(t, add_n)
        pass_near_on(t)
        return carry

    lax.fori_loop(0, 2, begin, 0)
    far_term(2, add_f)
    near_term(2, add_n)

    def step(t, carry):
        pass_far_on(t)
        far_term(t + 3, add_f)
        pass_near_on(t + 2)
        near_term(t + 3, add_n)

        @pl.when(t + slots < n - 2)
        def _():
            to_near(init_f.at[0], t + 2).wait_send()
            pl.semaphore_signal(free_f, inc=1, device_id={"tp": ring.far}, device_id_type=MESH)

        @pl.when((t >= 1) & (t - 1 + slots < n))
        def _():
            to_far(init_f.at[0], t - 1).wait_send()
            pl.semaphore_signal(free_n, inc=1, device_id={"tp": ring.near}, device_id_type=MESH)

        return carry

    lax.fori_loop(0, n - 4, step, 0)
    pass_far_on(n - 4)
    far_term(n - 1, add_f)
    finish_near(n - 2)
    near_term(n - 1, add_n)
    pass_far_on(n - 3)
    finish_near(n - 1)

    for t in range(2):
        to_near(init_f.at[0], t).wait_send()

    def finish(t, carry):
        to_near(init_f.at[0], t).wait_send()
        return carry

    lax.fori_loop(n - slots, n, finish, 0)

    def finish_far(t, carry):
        to_far(init_f.at[0], t).wait_send()
        return carry

    lax.fori_loop(n - slots, n - 2, finish_far, 0)


def ring_out(qkv, w_out, embed, b_out, n):
    _, half, width = embed.shape
    slots = n // 2
    dma = pltpu.SemaphoreType.DMA
    vmem = pl.BlockSpec(memory_space=pltpu.VMEM)
    return pl.pallas_call(
        functools.partial(ring_out_kernel, n, slots),
        out_shape=jax.ShapeDtypeStruct((2, half, width), BF16),
        in_specs=[vmem] * 4,
        out_specs=vmem,
        scratch_shapes=[
            pltpu.VMEM((2, half, width), F32),
            pltpu.VMEM((half, width), F32),
            pltpu.VMEM((half, width), F32),
            pltpu.VMEM((slots, half, width), F32),
            pltpu.VMEM((slots, half, width), F32),
            dma((n - 2,)), dma((n,)), dma((n - 2,)), dma((n,)),
            pltpu.SemaphoreType.REGULAR, pltpu.SemaphoreType.REGULAR,
        ],
        compiler_params=pltpu.CompilerParams(collective_id=3, has_side_effects=True, vmem_limit_bytes=VMEM_LIMIT),
        name="ring_out",
    )(qkv, w_out, embed, b_out)


def solution(mesh):
    n = mesh.shape["tp"]

    def local_step(token_ids, word_shard, pos_table, ln_gain, ln_bias, w_qkv, b_qkv, w_out, b_out):
        shard_rows, width = word_shard.shape
        seq_len = token_ids.shape[1]
        block_len = seq_len // n
        half = block_len // 2
        heads, head_dim = w_qkv.shape[2:]
        tp_index = lax.axis_index("tp")

        w = jnp.transpose(w_qkv, (1, 2, 3, 0)).reshape(3 * heads, head_dim, width)
        bias = b_qkv.reshape(3 * heads, 1, head_dim)

        local_ids = token_ids.reshape(seq_len) - tp_index * shard_rows
        partial_rows = gather_rows(local_ids, word_shard, block_len)
        block_rows = ring_sum(partial_rows.reshape(n, 2, half, width), n).reshape(block_len, width)
        pos_block = lax.dynamic_slice_in_dim(pos_table, tp_index * block_len, block_len, axis=0)
        embed = (block_rows.astype(F32) + pos_block.astype(F32)).astype(BF16)
        normed = layer_norm(embed.astype(F32), ln_gain, ln_bias).astype(BF16)
        qkv = ring_qkv(normed.reshape(2, half, width), w, bias, n)
        resid = ring_out(qkv.reshape(3 * heads, seq_len, 128), w_out, embed.reshape(2, half, width), b_out.reshape(1, width), n)
        return resid.reshape(1, block_len, width), embed.reshape(1, block_len, width)

    in_specs = (P("dp", None), P("tp", None), P(None, None), P(None), P(None), P(None, None, "tp", None), P(None, "tp", None), P("tp", None, None), P(None))
    out_specs = (P("dp", "tp", None), P("dp", "tp", None))
    return jax.shard_map(local_step, mesh=mesh, in_specs=in_specs, out_specs=out_specs, check_vma=False)
```

time: 912 us -> 575 us (0.63)
  waiting for transfers between devices: 603 us -> 0 us
  Pallas kernels: 0 us -> 564 us
  local copies, waits for them, and re-layouts: 140 us -> 3.62 us
  matrix products: 115 us -> 0 us
  other arithmetic: 37.6 us -> 6.39 us
  between operations: 13.9 us -> 0.72 us
    pallas_call x0 -> x4, Pallas kernels: none -> 564 us  [the longest x1 258 us: ring_out(): pl.pallas_call(functools.partial(ring_out_kernel, n, slots), out_shape=ja...]
    reduce_scatter x2 -> x0, waiting for transfers between devices: 476 us -> none  [the longest x1 264 us: local_step(): lax.psum_scatter(partial_out, 'tp', scatter_dimension=1, tiled=True)]
    gather x1 -> x0, local copies, waits for them, and re-layouts: 139 us -> none  [local_step(): table_rows = jnp.take(word_shard, local_ids, axis=0, mode='clip')]
    all_gather x1 -> x0, waiting for transfers between devices: 127 us -> none  [local_step(): normed = lax.all_gather(normed_block, 'tp', axis=1, tiled=True)]
    dot_general x2 -> x0, matrix products: 44.6 us -> none  [the longest x1 22.3 us: head_outputs(): jnp.einsum('bhqk,bhke->bhqe', attn_probs, projected[2], preferred_element...]
    sub x1 -> x0, matrix products: 35 us -> none  [head_outputs(): attn_probs = jax.nn.softmax(attn_scores, axis=-1).astype(jnp.bfloat16)]
    unnamed x1 -> x0, matrix products: 35 us -> none
    select_n x1 -> x0, other arithmetic: 21.6 us -> none  [local_step(): jnp.where(in_shard[:, :, None], table_rows, jnp.zeros((), jnp.bfloat16))]
  transfers between devices with their start and end apart: 3 -> 0, of which waited for: 3 -> 0; matrix products, arithmetic and copies ran while one was open for 0% -> 0% of each run, Pallas kernels for 0% -> 0%
where the time goes in v1:
time: 575 us
  Pallas kernels  564 us (98%)
  other arithmetic  6.39 us (1%)
    pallas_call x1, Pallas kernels, ring_out(): pl.pallas_call(functools.partial(ring_out_kernel, n, slots), out_shape=ja...  258 us
    pallas_call x1, Pallas kernels, ring_qkv(): pl.pallas_call(functools.partial(ring_qkv_kernel, n), out_shape=jax.Shape...  140 us
    pallas_call x1, Pallas kernels, ring_sum(): pl.pallas_call(functools.partial(ring_sum_kernel, n), out_shape=jax.Shape...  135 us
    pallas_call x1, Pallas kernels, gather_rows(): pl.pallas_call(functools.partial(gather_kernel, block_len, shard_rows), g...  32.2 us

profile of v1, /device:TPU:21, one launch (start us, length us, event | category | flops | bytes accessed | tf_op | source)
XLA Modules:
  0.0 575.0 jit_solution(804422940252030497)
XLA Ops:
  0.6 0.7 fusion.8
  1.3 0.7 broadcast_subtract_fusion
  2.0 0.4 copy.11.column_ref
  2.4 32.2 %gather_rows.1 = bf16[2048,6144]{1,0:T(8,128)(2,1)} custom-call(s32[2048]{0:T(1024)S(1)} %bitcast.18, s32[2048,1]{1,0:T(8,128)S(1)} %copy.11.column_ref, bf16[3152,6144]{1,0:T(8,128)(2,1)} %table_ref.1), custom_call_target="tpu_custom_call" | custom-call | tf_op jit(solution)/shard_map/gather_rows/pallas_call | solution.py:114
  34.6 134.9 %ring_sum.1 = bf16[2,64,6144]{2,1,0:T(8,128)(2,1)} custom-call(bf16[16,2,64,6144]{3,2,1,0:T(8,128)(2,1)} %bitcast.19), custom_call_target="tpu_custom_call" | custom-call | tf_op jit(solution)/shard_map/ring_sum/pallas_call | solution.py:239
  169.4 0.0 copy-start.1
  169.5 0.0 copy-start.2
  169.5 2.6 convert_reduce_fusion
  172.1 0.0 copy-start
  172.1 0.6 fusion.2
  172.7 0.5 copy-done
  173.2 0.0 copy-done.1
  173.2 0.0 copy-done.2
  173.2 1.8 fusion.5
  175.0 139.7 %ring_qkv.1 = bf16[12,16,2,64,128]{4,3,2,1,0:T(8,128)(2,1)} custom-call(bf16[2,64,6144]{2,1,0:T(8,128)(2,1)} %bitcast.24, bf16[12,96,6144]{2,1,0:T(8,128)(2,1)} %bitcast.23, f32[12,1,96]{2,1,0:T(1,128)} %bitcast.27), custom_call_target="tpu_custom_call" | custom-call | tf_op jit(solution)/shard_map/ring_qkv/pallas_call | solution.py:334
  314.7 257.5 %ring_out.1 = bf16[2,64,6144]{2,1,0:T(8,128)(2,1)} custom-call(bf16[12,2048,128]{2,1,0:T(8,128)(2,1)} %bitcast.22, bf16[4,96,6144]{2,1,0:T(8,128)(2,1)} %w_ref.1, bf16[2,64,6144]{2,1,0:T(8,128)(2,1)} %bitcast.20, f32[1,6144]{1,0:T(1,128)} %bitcast.26), custom_call_target="tpu_custom_call" | custom-call | tf_op jit(solution)/shard_map/ring_out/pallas_call | solution.py:477
  572.3 2.7 copy.13
  (2 shorter events, 0.0 us)
Async XLA Ops:
  169.4 3.8 copy-start.1
  169.5 3.8 copy-start.2
  172.1 1.1 copy-start

commit v2 on v1

--- a/solution.py
+++ b/solution.py
@@ -253,75 +253,80 @@
     )(partial_rows)
 
 
-def ring_qkv_kernel(n, own_ref, w_hbm, bias_ref, out_ref, w_ref, buf_n, buf_f, w_sem, send_f, send_n, recv_f, recv_n):
+def ring_qkv_kernel(n, own_hbm, w_hbm, bias_ref, out_ref, w_ref, buf, load_sem, send_f, send_n, recv_f, recv_n):
     ring = Ring(n)
-    half, width = own_ref.shape[1:]
+    _, _, half, width = buf.shape
     n_parts, part_width = w_ref.shape[:2]
-    load_w = pltpu.make_async_copy(w_hbm, w_ref, w_sem.at[0])
+    load_own = pltpu.make_async_copy(own_hbm, buf.at[0, pl.ds(2, 2)], load_sem.at[0])
+    load_own.start()
+    load_w = pltpu.make_async_copy(w_hbm, w_ref, load_sem.at[1])
     load_w.start()
     ring.barrier()
 
+    def near_slot(t):
+        return buf.at[lax.div(t, 2), lax.rem(t, 2)]
+
+    def far_slot(t):
+        return buf.at[lax.div(t, 2) + 1, 2 + lax.rem(t, 2)]
+
     def to_far(src, t):
-        return remote(src, buf_f.at[t], send_f.at[t], recv_f.at[t], ring.far)
+        return remote(src, far_slot(t), send_f.at[t], recv_f.at[t], ring.far)
 
     def to_near(src, t):
-        return remote(src, buf_n.at[t], send_n.at[t], recv_n.at[t], ring.near)
-
-    def multiply(rows, block, low, high):
+        return remote(src, near_slot(t), send_n.at[t], recv_n.at[t], ring.near)
+
+    def multiply(k, low, high):
+        near_owner = jnp.where(k == 0, ring.near, ring.near_block(k))
+        far_owner = jnp.where(k == 0, ring.me, ring.far_block(k))
+
         def one(c, carry):
             product = lax.dot_general(
-                rows[...].reshape(2 * half, width), w_ref[c], (((1,), (1,)), ((), ())), preferred_element_type=F32
+                buf[k].reshape(4 * half, width), w_ref[c], (((1,), (1,)), ((), ())), preferred_element_type=F32
             )
-            product = (product + bias_ref[c]).astype(BF16)
-            out_ref[c, block, :, :, :part_width] = product.reshape(2, half, part_width)
+            product = (product + bias_ref[c]).astype(BF16).reshape(2, 2, half, part_width)
+            out_ref[c, near_owner, :, :, :part_width] = product[0]
+            out_ref[c, far_owner, :, :, :part_width] = product[1]
             return carry
 
         lax.fori_loop(low, high, one, 0)
 
+    load_own.wait()
     for t in range(2):
-        to_far(own_ref.at[t], t).start()
+        to_far(buf.at[0, 2 + t], t).start()
     for t in range(2):
-        to_near(own_ref.at[t], t).start()
+        to_near(buf.at[0, 2 + t], t).start()
     out_ref[...] = jnp.zeros_like(out_ref)
+    for t in range(2):
+        to_near(near_slot(t), t).wait_recv()
     load_w.wait()
-    multiply(own_ref, ring.me, 0, n_parts)
-    for t in range(2):
-        to_near(buf_n.at[t], t).wait_recv()
-    mid = n_parts // 2
+    quarter = n_parts // 4
 
     def step(k, carry):
-        near_owner = jnp.where(k == 0, ring.near, ring.near_block(k))
         for h in range(2):
             t = 2 * k + h
-            to_far(buf_f.at[t], t).wait_recv()
-            to_near(buf_f.at[t], t + 2).start()
-            if h == 0:
-                multiply(buf_n.at[pl.ds(2 * k, 2)], near_owner, 0, mid)
-            else:
-                multiply(buf_f.at[pl.ds(2 * k, 2)], ring.far_block(k + 1), 0, mid)
-            to_near(buf_n.at[t + 2], t + 2).wait_recv()
+            to_far(far_slot(t), t).wait_recv()
+            to_near(far_slot(t), t + 2).start()
+            multiply(k, 2 * h * quarter, (2 * h + 1) * quarter)
+            to_near(near_slot(t + 2), t + 2).wait_recv()
 
             @pl.when(t + 2 < n - 2)
             def _():
-                to_far(buf_n.at[t + 2], t + 2).start()
-
-            if h == 0:
-                multiply(buf_n.at[pl.ds(2 * k, 2)], near_owner, mid, n_parts)
-            else:
-                multiply(buf_f.at[pl.ds(2 * k, 2)], ring.far_block(k + 1), mid, n_parts)
+                to_far(near_slot(t + 2), t + 2).start()
+
+            multiply(k, (2 * h + 1) * quarter, n_parts if h else 2 * quarter)
         return carry
 
     lax.fori_loop(0, n // 2 - 1, step, 0)
-    multiply(buf_n.at[pl.ds(n - 2, 2)], ring.near_block(n // 2 - 1), 0, n_parts)
+    multiply(n // 2 - 1, 0, n_parts)
 
     def finish(t, carry):
-        to_near(own_ref.at[0], t).wait_send()
+        to_near(buf.at[0, 0], t).wait_send()
         return carry
 
     lax.fori_loop(0, n, finish, 0)
 
     def finish_far(t, carry):
-        to_far(own_ref.at[0], t).wait_send()
+        to_far(buf.at[0, 0], t).wait_send()
         return carry
 
     lax.fori_loop(0, n - 2, finish_far, 0)
@@ -334,13 +339,12 @@
     return pl.pallas_call(
         functools.partial(ring_qkv_kernel, n),
         out_shape=jax.ShapeDtypeStruct((w.shape[0], n, 2, half, 128), BF16),
-        in_specs=[vmem, pl.BlockSpec(memory_space=pl.ANY), vmem],
+        in_specs=[pl.BlockSpec(memory_space=pl.ANY), pl.BlockSpec(memory_space=pl.ANY), vmem],
         out_specs=vmem,
         scratch_shapes=[
             pltpu.VMEM(w.shape, BF16),
-            pltpu.VMEM((n, half, width), BF16),
-            pltpu.VMEM((n - 2, half, width), BF16),
-            dma((1,)), dma((n - 2,)), dma((n,)), dma((n - 2,)), dma((n,)),
+            pltpu.VMEM((n // 2, 4, half, width), BF16),
+            dma((2,)), dma((n - 2,)), dma((n,)), dma((n - 2,)), dma((n,)),
         ],
         compiler_params=pltpu.CompilerParams(collective_id=2, has_side_effects=True, vmem_limit_bytes=VMEM_LIMIT),
         name="ring_qkv",
@@ -493,11 +497,163 @@
     )(qkv, w_out, embed, b_out)
 
 
+LIMIT = 16
+
+
+def pick_kernel(want_ref, column_ref, table_ref, out_ref, fetched, sems):
+    j = pl.program_id(0)
+
+    def each(block, slot, act):
+        def one(k, carry):
+            row = want_ref[block * LIMIT + k]
+
+            @pl.when(row >= 0)
+            def _():
+                start = pl.multiple_of(lax.div(row, ROWS) * ROWS, ROWS)
+                act(pltpu.make_async_copy(
+                    table_ref.at[pl.ds(start, ROWS), :],
+                    fetched.at[slot, pl.ds(pl.multiple_of(k * ROWS, ROWS), ROWS), :],
+                    sems.at[slot, k],
+                ))
+
+            return carry
+
+        lax.fori_loop(0, LIMIT, one, 0)
+
+    @pl.when(j == 0)
+    def _():
+        fetched[...] = jnp.zeros_like(fetched)
+        each(0, 0, lambda copy: copy.start())
+
+    @pl.when(j + 1 < pl.num_programs(0))
+    def _():
+        each(j + 1, lax.rem(j + 1, 2), lambda copy: copy.start())
+
+    slot = lax.rem(j, 2)
+    columns = lax.broadcasted_iota(jnp.int32, (LIMIT, LIMIT * ROWS), 1)
+    place = lax.broadcasted_iota(jnp.int32, (LIMIT, LIMIT * ROWS), 0) * ROWS
+    row = column_ref[...]
+    selector = jnp.where((row >= 0) & (columns == place + lax.rem(jnp.maximum(row, 0), ROWS)), 1.0, 0.0).astype(BF16)
+    each(j, slot, lambda copy: copy.wait())
+    out_ref[...] = jnp.dot(selector, fetched[slot], preferred_element_type=F32).astype(BF16)
+
+
+def pick_rows(want, table, n):
+    width = table.shape[1]
+    return pl.pallas_call(
+        pick_kernel,
+        grid=(n,),
+        out_shape=jax.ShapeDtypeStruct((n * LIMIT, width), BF16),
+        in_specs=[
+            pl.BlockSpec(memory_space=pltpu.SMEM),
+            pl.BlockSpec((LIMIT, 1), lambda j: (j, 0)),
+            pl.BlockSpec(memory_space=pl.ANY),
+        ],
+        out_specs=pl.BlockSpec((LIMIT, width), lambda j: (j, 0)),
+        scratch_shapes=[pltpu.VMEM((2, LIMIT * ROWS, width), BF16), pltpu.SemaphoreType.DMA((2, LIMIT))],
+        compiler_params=pltpu.CompilerParams(vmem_limit_bytes=VMEM_LIMIT),
+        name="pick_rows",
+    )(want, want.reshape(n * LIMIT, 1), table)
+
+
+def exchange_kernel(n, picked_ref, index_ref, out_ref, got, own_sem, send, recv):
+    me = lax.axis_index("tp")
+    own = pltpu.make_async_copy(picked_ref.at[me], got.at[me], own_sem.at[0])
+    own.start()
+    barrier = pltpu.get_barrier_semaphore()
+
+    def greet(j, carry):
+        pl.semaphore_signal(barrier, inc=1, device_id={"tp": lax.rem(me + j, n)}, device_id_type=MESH)
+        return carry
+
+    lax.fori_loop(1, n, greet, 0)
+    pl.semaphore_wait(barrier, n - 1)
+
+    def copy_to(j):
+        other = lax.rem(me + j, n)
+        return remote(picked_ref.at[other], got.at[me], send.at[j], recv.at[j], other)
+
+    for j in range(n // 2, 0, -1):
+        copy_to(j).start()
+        if j < n // 2:
+            copy_to(n - j).start()
+
+    def arrive(j, carry):
+        source = lax.rem(me - j + n, n)
+        remote(picked_ref.at[0], got.at[source], send.at[j], recv.at[j], source).wait_recv()
+        return carry
+
+    lax.fori_loop(1, n, arrive, 0)
+    own.wait()
+    block_len, width = out_ref.shape
+    rows = n * LIMIT
+    selector = jnp.where(lax.broadcasted_iota(jnp.int32, (block_len, rows), 1) == index_ref[...], 1.0, 0.0).astype(BF16)
+    chunk = width // 4
+    for c in range(4):
+        columns = slice(c * chunk, (c + 1) * chunk)
+        out_ref[:, columns] = jnp.dot(
+            selector, got[:, :, columns].reshape(rows, chunk), preferred_element_type=F32
+        ).astype(BF16)
+
+    def sent(j, carry):
+        copy_to(j).wait_send()
+        return carry
+
+    lax.fori_loop(1, n, sent, 0)
+
+
+def exchange(picked, index, n):
+    _, _, width = picked.shape
+    dma = pltpu.SemaphoreType.DMA
+    vmem = pl.BlockSpec(memory_space=pltpu.VMEM)
+    return pl.pallas_call(
+        functools.partial(exchange_kernel, n),
+        out_shape=jax.ShapeDtypeStruct((index.shape[0], width), BF16),
+        in_specs=[pl.BlockSpec(memory_space=pl.ANY), vmem],
+        out_specs=vmem,
+        scratch_shapes=[pltpu.VMEM((n, LIMIT, width), BF16), dma((1,)), dma((n,)), dma((n,))],
+        compiler_params=pltpu.CompilerParams(collective_id=4, has_side_effects=True, vmem_limit_bytes=VMEM_LIMIT),
+        name="exchange",
+    )(picked, index)
+
+
+def look_up(token_ids, table, n):
+    shard_rows, width = table.shape
+    me = lax.axis_index("tp")
+    ids = token_ids.reshape(n, -1)
+    block_len = ids.shape[1]
+    earlier = lax.broadcasted_iota(jnp.int32, (block_len, block_len), 0) > lax.broadcasted_iota(jnp.int32, (block_len, block_len), 1)
+    same = ids[:, :, None] == ids[:, None, :]
+    fresh = jnp.sum((same & earlier[None]).astype(jnp.int32), axis=2) == 0
+    owner = lax.div(ids, shard_rows)
+    rank = jnp.sum(((owner[:, :, None] == owner[:, None, :]) & earlier[None] & fresh[:, None, :]).astype(jnp.int32), axis=2)
+    overflow = jnp.max(jnp.where(fresh, rank, 0)) >= LIMIT
+    places = lax.broadcasted_iota(jnp.int32, (n, LIMIT, block_len), 1)
+    wanted = (places == rank[:, None, :]) & (fresh & (owner == me))[:, None, :]
+    want = jnp.sum(jnp.where(wanted, (ids - me * shard_rows)[:, None, :] + 1, 0), axis=2) - 1
+
+    my_ids = lax.dynamic_index_in_dim(ids, me, 0, keepdims=False)
+    my_slots = lax.dynamic_index_in_dim(jnp.where(fresh, owner * LIMIT + rank, 0), me, 0, keepdims=False)
+    my_fresh = lax.dynamic_index_in_dim(fresh, me, 0, keepdims=False)
+    match = (my_ids[:, None] == my_ids[None, :]) & my_fresh[None, :]
+    index = jnp.sum(jnp.where(match, my_slots[None, :], 0), axis=1)
+
+    def by_exchange():
+        return exchange(pick_rows(want.reshape(n * LIMIT), table, n).reshape(n, LIMIT, width), index.reshape(block_len, 1), n)
+
+    def by_sum():
+        local_ids = token_ids.reshape(n * block_len) - me * shard_rows
+        partial_rows = gather_rows(local_ids, table, block_len)
+        return ring_sum(partial_rows.reshape(n, 2, block_len // 2, width), n).reshape(block_len, width)
+
+    return lax.cond(overflow, by_sum, by_exchange)
+
+
 def solution(mesh):
     n = mesh.shape["tp"]
 
     def local_step(token_ids, word_shard, pos_table, ln_gain, ln_bias, w_qkv, b_qkv, w_out, b_out):
-        shard_rows, width = word_shard.shape
+        width = word_shard.shape[1]
         seq_len = token_ids.shape[1]
         block_len = seq_len // n
         half = block_len // 2
@@ -507,9 +663,7 @@
         w = jnp.transpose(w_qkv, (1, 2, 3, 0)).reshape(3 * heads, head_dim, width)
         bias = b_qkv.reshape(3 * heads, 1, head_dim)
 
-        local_ids = token_ids.reshape(seq_len) - tp_index * shard_rows
-        partial_rows = gather_rows(local_ids, word_shard, block_len)
-        block_rows = ring_sum(partial_rows.reshape(n, 2, half, width), n).reshape(block_len, width)
+        block_rows = look_up(token_ids.reshape(seq_len), word_shard, n)
         pos_block = lax.dynamic_slice_in_dim(pos_table, tp_index * block_len, block_len, axis=0)
         embed = (block_rows.astype(F32) + pos_block.astype(F32)).astype(BF16)
         normed = layer_norm(embed.astype(F32), ln_gain, ln_bias).astype(BF16)

time: 575 us -> 521 us (0.906)
  Pallas kernels: 564 us -> 501 us
    pallas_call x2, Pallas kernels: 167 us -> 102 us  [the longest x1 83 us: exchange(): pl.pallas_call(functools.partial(exchange_kernel, n), out_shape=jax.Shape...]
where the time goes in v2:
time: 521 us; the launch traced here: 519 us
  Pallas kernels  501 us (96%)
  other arithmetic  11.1 us (2%)
  local copies, waits for them, and re-layouts  5.45 us (1%)
    pallas_call x1, Pallas kernels, ring_out(): pl.pallas_call(functools.partial(ring_out_kernel, n, slots), out_shape=ja...  256 us
    pallas_call x1, Pallas kernels, ring_qkv(): pl.pallas_call(functools.partial(ring_qkv_kernel, n), out_shape=jax.Shape...  143 us
    pallas_call x1, Pallas kernels, exchange(): pl.pallas_call(functools.partial(exchange_kernel, n), out_shape=jax.Shape...  83 us
    pallas_call x1, Pallas kernels, pick_rows(): pl.pallas_call(pick_kernel, grid=(n,), out_shape=jax.ShapeDtypeStruct((n...  18.5 us

profile of v2, /device:TPU:21, one launch (start us, length us, event | category | flops | bytes accessed | tf_op | source)
XLA Modules:
  0.0 519.5 jit_solution(15556004646340275848)
XLA Ops:
  0.7 1.4 convert_reduce_fusion.2
  2.1 0.7 broadcast_divide_fusion
  2.8 0.6 convert_reduce_fusion.1
  3.5 0.6 select_reduce_fusion.2
  4.8 106.7 %conditional.2 = (bf16[128,6144]{1,0:T(8,128)(2,1)}) conditional(s32[]{:T(128)} %convert_element_type.32, (s32[16,128]{1,0:T(8,128)S(1)}, s32[16,16,128]{2,1,0:T(8,128)S(1)}, s32[16,128]{1,0:T(8,128)S(1)}, s32[1,2048]{1,0:T(1,128)}, s32[]{:T(128)}, /*index=5*/bf16[3152,6144]{1,0:T(8,128)(2,1)}, s32[16,128]{1,0:T(8,128)}, ...), branch_computations={%region_3.0_spmd, %region_6.7_spmd} | conditional | flops 209284 | bytes 201286
  4.8 0.7 fusion.4
  5.5 0.2 select_reduce_fusion.1
  5.7 0.8 copy.16.index_ref
  6.4 0.7 subtract_add_fusion
  7.1 0.8 compare_reduce_fusion
  7.9 0.4 select_reduce_fusion
  8.3 0.8 sub.43.column_ref
  9.0 0.7 sub.33.want_ref
  9.7 18.5 %pick_rows.4 = bf16[256,6144]{1,0:T(8,128)(2,1)} custom-call(s32[256]{0:T(256)} %sub.33.want_ref, s32[256,1]{1,0:T(8,128)} %sub.43.column_ref, bf16[3152,6144]{1,0:T(8,128)(2,1)} %get-tuple-element.250.table_ref), custom_call_target="tpu_custom_call" | custom-call | tf_op jit(solution)/shard_map/cond/branch_0_fun/pick_rows/pallas_call | solution.py:543
  28.2 83.0 %exchange.4 = bf16[128,6144]{1,0:T(8,128)(2,1)} custom-call(bf16[16,16,6144]{2,1,0:T(8,128)(2,1)} %bitcast.33, s32[128,1]{1,0:T(8,128)} %copy.16.index_ref), custom_call_target="tpu_custom_call" | custom-call | tf_op jit(solution)/shard_map/cond/branch_0_fun/exchange/pallas_call | solution.py:609
  111.4 0.0 copy-start.1
  111.4 0.0 copy-start.2
  111.4 2.6 convert_reduce_fusion
  114.0 0.0 copy-start
  114.1 0.6 fusion.7
  114.6 0.5 copy-done
  115.2 0.0 copy-done.1
  115.2 0.0 copy-done.2
  115.2 1.8 fusion.10
  117.0 143.4 %ring_qkv.1 = bf16[12,16,2,64,128]{4,3,2,1,0:T(8,128)(2,1)} custom-call(bf16[2,64,6144]{2,1,0:T(8,128)(2,1)} %bitcast.35, bf16[12,96,6144]{2,1,0:T(8,128)(2,1)} %bitcast.32, f32[12,1,96]{2,1,0:T(1,128)} %bitcast.44), custom_call_target="tpu_custom_call" | custom-call | tf_op jit(solution)/shard_map/ring_qkv/pallas_call | solution.py:339
  260.4 256.4 %ring_out.1 = bf16[2,64,6144]{2,1,0:T(8,128)(2,1)} custom-call(bf16[12,2048,128]{2,1,0:T(8,128)(2,1)} %bitcast.31, bf16[4,96,6144]{2,1,0:T(8,128)(2,1)} %w_ref.1, bf16[2,64,6144]{2,1,0:T(8,128)(2,1)} %bitcast.29, f32[1,6144]{1,0:T(1,128)} %bitcast.43), custom_call_target="tpu_custom_call" | custom-call | tf_op jit(solution)/shard_map/ring_out/pallas_call | solution.py:481
  516.8 2.7 copy.21
  (9 shorter events, 0.1 us)
Async XLA Ops:
  111.4 3.8 copy-start.1
  111.4 3.8 copy-start.2
  114.0 1.1 copy-start

commit v3 on v2

--- a/solution.py
+++ b/solution.py
@@ -253,10 +253,11 @@
     )(partial_rows)
 
 
-def ring_qkv_kernel(n, own_hbm, w_hbm, bias_ref, out_ref, w_ref, buf, load_sem, send_f, send_n, recv_f, recv_n):
+def ring_qkv_kernel(n, pack, own_hbm, w_hbm, bias_ref, out_ref, w_ref, buf, load_sem, send_f, send_n, recv_f, recv_n):
     ring = Ring(n)
     _, _, half, width = buf.shape
     n_parts, part_width = w_ref.shape[:2]
+    head_dim = part_width // pack
     load_own = pltpu.make_async_copy(own_hbm, buf.at[0, pl.ds(2, 2)], load_sem.at[0])
     load_own.start()
     load_w = pltpu.make_async_copy(w_hbm, w_ref, load_sem.at[1])
@@ -283,9 +284,11 @@
             product = lax.dot_general(
                 buf[k].reshape(4 * half, width), w_ref[c], (((1,), (1,)), ((), ())), preferred_element_type=F32
             )
-            product = (product + bias_ref[c]).astype(BF16).reshape(2, 2, half, part_width)
-            out_ref[c, near_owner, :, :, :part_width] = product[0]
-            out_ref[c, far_owner, :, :, :part_width] = product[1]
+            product = (product + bias_ref[c]).astype(BF16)
+            for i in range(pack):
+                piece = product[:, i * head_dim:(i + 1) * head_dim].reshape(2, 2, half, head_dim)
+                out_ref[pack * c + i, near_owner, :, :, :head_dim] = piece[0]
+                out_ref[pack * c + i, far_owner, :, :, :head_dim] = piece[1]
             return carry
 
         lax.fori_loop(low, high, one, 0)
@@ -299,21 +302,21 @@
     for t in range(2):
         to_near(near_slot(t), t).wait_recv()
     load_w.wait()
-    quarter = n_parts // 4
+    cut = [n_parts * i // 4 for i in range(5)]
 
     def step(k, carry):
         for h in range(2):
             t = 2 * k + h
             to_far(far_slot(t), t).wait_recv()
             to_near(far_slot(t), t + 2).start()
-            multiply(k, 2 * h * quarter, (2 * h + 1) * quarter)
+            multiply(k, cut[2 * h], cut[2 * h + 1])
             to_near(near_slot(t + 2), t + 2).wait_recv()
 
             @pl.when(t + 2 < n - 2)
             def _():
                 to_far(near_slot(t + 2), t + 2).start()
 
-            multiply(k, (2 * h + 1) * quarter, n_parts if h else 2 * quarter)
+            multiply(k, cut[2 * h + 1], cut[2 * h + 2])
         return carry
 
     lax.fori_loop(0, n // 2 - 1, step, 0)
@@ -332,13 +335,13 @@
     lax.fori_loop(0, n - 2, finish_far, 0)
 
 
-def ring_qkv(normed, w, bias, n):
+def ring_qkv(normed, w, bias, n, pack):
     _, half, width = normed.shape
     dma = pltpu.SemaphoreType.DMA
     vmem = pl.BlockSpec(memory_space=pltpu.VMEM)
     return pl.pallas_call(
-        functools.partial(ring_qkv_kernel, n),
-        out_shape=jax.ShapeDtypeStruct((w.shape[0], n, 2, half, 128), BF16),
+        functools.partial(ring_qkv_kernel, n, pack),
+        out_shape=jax.ShapeDtypeStruct((pack * w.shape[0], n, 2, half, 128), BF16),
         in_specs=[pl.BlockSpec(memory_space=pl.ANY), pl.BlockSpec(memory_space=pl.ANY), vmem],
         out_specs=vmem,
         scratch_shapes=[
@@ -351,7 +354,7 @@
     )(normed, w, bias)
 
 
-def ring_out_kernel(n, slots, qkv_ref, w_ref, embed_ref, bias_ref, out_ref, init_f, add_n, add_f, buf_n, buf_f,
+def ring_out_kernel(n, slots, qkv_ref, w_hbm, embed_hbm, bias_ref, out_ref, w_ref, embed_ref, load_sem, init_f, add_n, add_f, buf_n, buf_f,
                     send_f, send_n, recv_f, recv_n, free_f, free_n):
     ring = Ring(n)
     heads, head_dim, width = w_ref.shape
@@ -359,13 +362,21 @@
     seq_len = qkv_ref.shape[1]
     chunk = width // 4
     scale = head_dim ** -0.5
-
-    def term(block, which, dst):
-        first = pl.multiple_of((block * 2 + which) * half, half)
-        visible = lax.broadcasted_iota(jnp.int32, (half, seq_len), 1) <= first + lax.broadcasted_iota(jnp.int32, (half, seq_len), 0)
+    load_w = pltpu.make_async_copy(w_hbm, w_ref, load_sem.at[0])
+    load_w.start()
+    load_embed = pltpu.make_async_copy(embed_hbm, embed_ref, load_sem.at[1])
+    load_embed.start()
+
+    def term(places):
+        firsts = [pl.multiple_of((block * 2 + which) * half, half) for block, which, _ in places]
+        key = lax.broadcasted_iota(jnp.int32, (half, seq_len), 1)
+        row = lax.broadcasted_iota(jnp.int32, (half, seq_len), 0)
+        visible = jnp.concatenate([key - row for _ in places], axis=0) <= jnp.concatenate(
+            [jnp.full((half, 1), first, jnp.int32) for first in firsts], axis=0
+        )
         contexts = []
         for h in range(heads):
-            query = qkv_ref[h, pl.ds(first, half), :]
+            query = jnp.concatenate([qkv_ref[h, pl.ds(first, half), :] for first in firsts], axis=0)
             scores = lax.dot_general(query, qkv_ref[heads + h], (((1,), (1,)), ((), ())), preferred_element_type=F32) * scale
             scores = jnp.where(visible, scores, -jnp.inf)
             scores = jnp.exp(scores - jnp.max(scores, axis=-1, keepdims=True))
@@ -377,13 +388,20 @@
             total = jnp.dot(contexts[0], w_ref[0, :, columns], preferred_element_type=F32)
             for h in range(1, heads):
                 total += jnp.dot(contexts[h], w_ref[h, :, columns], preferred_element_type=F32)
-            dst[:, columns] = total
+            for i, (_, _, dst) in enumerate(places):
+                dst[:, columns] = total[i * half:(i + 1) * half]
+
+    def near_place(t, dst):
+        return ring.near_block(lax.div(t, 2) + 1), lax.rem(t, 2), dst
+
+    def far_place(t, dst):
+        return ring.far_block(lax.div(t, 2) + 1), lax.rem(t, 2), dst
 
     def near_term(t, dst):
-        term(ring.near_block(lax.div(t, 2) + 1), lax.rem(t, 2), dst)
+        term([near_place(t, dst)])
 
     def far_term(t, dst):
-        term(ring.far_block(lax.div(t, 2) + 1), lax.rem(t, 2), dst)
+        term([far_place(t, dst)])
 
     def to_far(src, t):
         return remote(src, buf_f.at[lax.rem(t, slots)], send_f.at[t], recv_f.at[t], ring.far)
@@ -420,16 +438,25 @@
 
     ring.barrier()
 
+    load_w.wait()
+
+    def pair(t, dst):
+        term([far_place(t, dst), near_place(t, add_n)])
+
     def begin(t, carry):
-        far_term(t, init_f.at[t])
-        to_near(init_f.at[t], t).start()
-        near_term(t, add_n)
-        pass_near_on(t)
-        return carry
-
-    lax.fori_loop(0, 2, begin, 0)
-    far_term(2, add_f)
-    near_term(2, add_n)
+        pair(t, init_f.at[t])
+
+        @pl.when(t < 2)
+        def _():
+            to_near(init_f.at[t], t).start()
+            pass_near_on(t)
+
+        return carry
+
+    lax.fori_loop(0, 3, begin, 0)
+    load_embed.wait()
+
+    add_f[...] = init_f[2]
 
     def step(t, carry):
         pass_far_on(t)
@@ -481,10 +508,13 @@
     return pl.pallas_call(
         functools.partial(ring_out_kernel, n, slots),
         out_shape=jax.ShapeDtypeStruct((2, half, width), BF16),
-        in_specs=[vmem] * 4,
+        in_specs=[vmem, pl.BlockSpec(memory_space=pl.ANY), pl.BlockSpec(memory_space=pl.ANY), vmem],
         out_specs=vmem,
         scratch_shapes=[
-            pltpu.VMEM((2, half, width), F32),
+            pltpu.VMEM(w_out.shape, BF16),
+            pltpu.VMEM((2, half, width), BF16),
+            dma((2,)),
+            pltpu.VMEM((3, half, width), F32),
             pltpu.VMEM((half, width), F32),
             pltpu.VMEM((half, width), F32),
             pltpu.VMEM((slots, half, width), F32),
@@ -498,6 +528,7 @@
 
 
 LIMIT = 16
+GROUP = 8
 
 
 def pick_kernel(want_ref, column_ref, table_ref, out_ref, fetched, sems):
@@ -509,10 +540,10 @@
 
             @pl.when(row >= 0)
             def _():
-                start = pl.multiple_of(lax.div(row, ROWS) * ROWS, ROWS)
+                start = pl.multiple_of(lax.div(row, GROUP) * GROUP, GROUP)
                 act(pltpu.make_async_copy(
-                    table_ref.at[pl.ds(start, ROWS), :],
-                    fetched.at[slot, pl.ds(pl.multiple_of(k * ROWS, ROWS), ROWS), :],
+                    table_ref.at[pl.ds(start, GROUP), :],
+                    fetched.at[slot, k],
                     sems.at[slot, k],
                 ))
 
@@ -530,12 +561,12 @@
         each(j + 1, lax.rem(j + 1, 2), lambda copy: copy.start())
 
     slot = lax.rem(j, 2)
-    columns = lax.broadcasted_iota(jnp.int32, (LIMIT, LIMIT * ROWS), 1)
-    place = lax.broadcasted_iota(jnp.int32, (LIMIT, LIMIT * ROWS), 0) * ROWS
+    columns = lax.broadcasted_iota(jnp.int32, (LIMIT, LIMIT * GROUP), 1)
+    place = lax.broadcasted_iota(jnp.int32, (LIMIT, LIMIT * GROUP), 0) * GROUP
     row = column_ref[...]
-    selector = jnp.where((row >= 0) & (columns == place + lax.rem(jnp.maximum(row, 0), ROWS)), 1.0, 0.0).astype(BF16)
+    selector = jnp.where((row >= 0) & (columns == place + lax.rem(jnp.maximum(row, 0), GROUP)), 1.0, 0.0).astype(BF16)
     each(j, slot, lambda copy: copy.wait())
-    out_ref[...] = jnp.dot(selector, fetched[slot], preferred_element_type=F32).astype(BF16)
+    out_ref[...] = jnp.dot(selector, fetched[slot].reshape(LIMIT * GROUP, out_ref.shape[1]), preferred_element_type=F32).astype(BF16)
 
 
 def pick_rows(want, table, n):
@@ -550,7 +581,7 @@
             pl.BlockSpec(memory_space=pl.ANY),
         ],
         out_specs=pl.BlockSpec((LIMIT, width), lambda j: (j, 0)),
-        scratch_shapes=[pltpu.VMEM((2, LIMIT * ROWS, width), BF16), pltpu.SemaphoreType.DMA((2, LIMIT))],
+        scratch_shapes=[pltpu.VMEM((2, LIMIT, GROUP, width), BF16), pltpu.SemaphoreType.DMA((2, LIMIT))],
         compiler_params=pltpu.CompilerParams(vmem_limit_bytes=VMEM_LIMIT),
         name="pick_rows",
     )(want, want.reshape(n * LIMIT, 1), table)
@@ -660,14 +691,15 @@
         heads, head_dim = w_qkv.shape[2:]
         tp_index = lax.axis_index("tp")
 
-        w = jnp.transpose(w_qkv, (1, 2, 3, 0)).reshape(3 * heads, head_dim, width)
-        bias = b_qkv.reshape(3 * heads, 1, head_dim)
+        pack = 2 if heads % 2 == 0 else 1
+        w = jnp.transpose(w_qkv, (1, 2, 3, 0)).reshape(3 * heads // pack, pack * head_dim, width)
+        bias = b_qkv.reshape(3 * heads // pack, 1, pack * head_dim)
 
         block_rows = look_up(token_ids.reshape(seq_len), word_shard, n)
         pos_block = lax.dynamic_slice_in_dim(pos_table, tp_index * block_len, block_len, axis=0)
         embed = (block_rows.astype(F32) + pos_block.astype(F32)).astype(BF16)
         normed = layer_norm(embed.astype(F32), ln_gain, ln_bias).astype(BF16)
-        qkv = ring_qkv(normed.reshape(2, half, width), w, bias, n)
+        qkv = ring_qkv(normed.reshape(2, half, width), w, bias, n, pack)
         resid = ring_out(qkv.reshape(3 * heads, seq_len, 128), w_out, embed.reshape(2, half, width), b_out.reshape(1, width), n)
         return resid.reshape(1, block_len, width), embed.reshape(1, block_len, width)
 

time: 521 us -> 510 us (0.979)
  Pallas kernels: 501 us -> 491 us
    pallas_call x1, Pallas kernels: 143 us -> 136 us  [ring_qkv(): pl.pallas_call(functools.partial(ring_qkv_kernel, n, pack), out_shape=jax...]
where the time goes in v3:
time: 510 us
  Pallas kernels  491 us (96%)
  other arithmetic  11.1 us (2%)
  local copies, waits for them, and re-layouts  6.12 us (1%)
    pallas_call x1, Pallas kernels, ring_out(): pl.pallas_call(functools.partial(ring_out_kernel, n, slots), out_shape=ja...  257 us
    pallas_call x1, Pallas kernels, ring_qkv(): pl.pallas_call(functools.partial(ring_qkv_kernel, n, pack), out_shape=jax...  136 us
    pallas_call x1, Pallas kernels, exchange(): pl.pallas_call(functools.partial(exchange_kernel, n), out_shape=jax.Shape...  81.8 us
    pallas_call x1, Pallas kernels, pick_rows(): pl.pallas_call(pick_kernel, grid=(n,), out_shape=jax.ShapeDtypeStruct((n...  15.4 us

profile of v3, /device:TPU:21, one launch (start us, length us, event | category | flops | bytes accessed | tf_op | source)
XLA Modules:
  0.0 509.6 jit_solution(5071948444104851466)
XLA Ops:
  0.7 1.4 convert_reduce_fusion.2
  2.1 0.7 broadcast_divide_fusion
  2.8 0.6 convert_reduce_fusion.1
  3.5 0.6 select_reduce_fusion.2
  4.8 102.3 %conditional.2 = (bf16[128,6144]{1,0:T(8,128)(2,1)}) conditional(s32[]{:T(128)} %convert_element_type.32, (s32[16,128]{1,0:T(8,128)S(1)}, s32[16,16,128]{2,1,0:T(8,128)S(1)}, s32[16,128]{1,0:T(8,128)S(1)}, s32[1,2048]{1,0:T(1,128)}, s32[]{:T(128)}, /*index=5*/bf16[3152,6144]{1,0:T(8,128)(2,1)}, s32[16,128]{1,0:T(8,128)}, ...), branch_computations={%region_3.0_spmd, %region_6.7_spmd} | conditional | flops 209284 | bytes 201286
  4.8 0.7 fusion.4
  5.5 0.2 select_reduce_fusion.1
  5.7 0.8 copy.16.index_ref
  6.4 0.7 subtract_add_fusion
  7.1 0.8 compare_reduce_fusion
  7.9 0.4 select_reduce_fusion
  8.3 0.8 sub.43.column_ref
  9.0 0.7 sub.33.want_ref
  9.7 15.4 %pick_rows.4 = bf16[256,6144]{1,0:T(8,128)(2,1)} custom-call(s32[256]{0:T(256)} %sub.33.want_ref, s32[256,1]{1,0:T(8,128)} %sub.43.column_ref, bf16[3152,6144]{1,0:T(8,128)(2,1)} %get-tuple-element.250.table_ref), custom_call_target="tpu_custom_call" | custom-call | tf_op jit(solution)/shard_map/cond/branch_0_fun/pick_rows/pallas_call | solution.py:574
  25.1 81.8 %exchange.4 = bf16[128,6144]{1,0:T(8,128)(2,1)} custom-call(bf16[16,16,6144]{2,1,0:T(8,128)(2,1)} %bitcast.32, s32[128,1]{1,0:T(8,128)} %copy.16.index_ref), custom_call_target="tpu_custom_call" | custom-call | tf_op jit(solution)/shard_map/cond/branch_0_fun/exchange/pallas_call | solution.py:640
  107.1 0.0 copy-start.1
  107.1 0.0 copy-start.2
  107.1 2.6 convert_reduce_fusion
  109.7 0.0 copy-start
  109.7 0.0 copy-start.3
  109.8 0.6 fusion.7
  110.3 0.5 copy-done
  110.9 0.0 copy-done.1
  110.9 0.0 copy-done.2
  110.9 1.8 fusion.10
  112.7 0.0 copy-done.3
  112.7 0.7 reshape.141.bias_ref
  113.4 136.3 %ring_qkv.1 = bf16[12,16,2,64,128]{4,3,2,1,0:T(8,128)(2,1)} custom-call(bf16[2,64,6144]{2,1,0:T(8,128)(2,1)} %bitcast.34, bf16[6,192,6144]{2,1,0:T(8,128)(2,1)} %bitcast.31, f32[6,1,192]{2,1,0:T(1,128)} %reshape.141.bias_ref), custom_call_target="tpu_custom_call" | custom-call | tf_op jit(solution)/shard_map/ring_qkv/pallas_call | solution.py:342
  249.7 257.2 %ring_out.1 = bf16[2,64,6144]{2,1,0:T(8,128)(2,1)} custom-call(bf16[12,2048,128]{2,1,0:T(8,128)(2,1)} %bitcast.30, bf16[4,96,6144]{2,1,0:T(8,128)(2,1)} %w_hbm.1, bf16[2,64,6144]{2,1,0:T(8,128)(2,1)} %bitcast.28, f32[1,6144]{1,0:T(1,128)} %bitcast.42), custom_call_target="tpu_custom_call" | custom-call | tf_op jit(solution)/shard_map/ring_out/pallas_call | solution.py:508
  506.9 2.7 copy.21
  (9 shorter events, 0.1 us)
Async XLA Ops:
  107.1 3.8 copy-start.1
  107.1 3.8 copy-start.2
  109.7 1.1 copy-start
  109.7 3.0 copy-start.3

commit v4 on v3

--- a/solution.py
+++ b/solution.py
@@ -354,7 +354,7 @@
     )(normed, w, bias)
 
 
-def ring_out_kernel(n, slots, qkv_ref, w_hbm, embed_hbm, bias_ref, out_ref, w_ref, embed_ref, load_sem, init_f, add_n, add_f, buf_n, buf_f,
+def ring_out_kernel(n, slots, qkv_hbm, w_hbm, embed_hbm, bias_ref, out_ref, qkv_ref, w_ref, embed_ref, load_sem, init_f, add_n, add_f, buf_n, buf_f,
                     send_f, send_n, recv_f, recv_n, free_f, free_n):
     ring = Ring(n)
     heads, head_dim, width = w_ref.shape
@@ -362,6 +362,8 @@
     seq_len = qkv_ref.shape[1]
     chunk = width // 4
     scale = head_dim ** -0.5
+    load_qkv = pltpu.make_async_copy(qkv_hbm, qkv_ref, load_sem.at[2])
+    load_qkv.start()
     load_w = pltpu.make_async_copy(w_hbm, w_ref, load_sem.at[0])
     load_w.start()
     load_embed = pltpu.make_async_copy(embed_hbm, embed_ref, load_sem.at[1])
@@ -437,7 +439,7 @@
         out_ref[t % 2] = (embed_ref[t % 2].astype(F32) + (buf_n[slot] + add_n[...]) + bias_ref[...]).astype(BF16)
 
     ring.barrier()
-
+    load_qkv.wait()
     load_w.wait()
 
     def pair(t, dst):
@@ -508,12 +510,13 @@
     return pl.pallas_call(
         functools.partial(ring_out_kernel, n, slots),
         out_shape=jax.ShapeDtypeStruct((2, half, width), BF16),
-        in_specs=[vmem, pl.BlockSpec(memory_space=pl.ANY), pl.BlockSpec(memory_space=pl.ANY), vmem],
+        in_specs=[pl.BlockSpec(memory_space=pl.ANY)] * 3 + [vmem],
         out_specs=vmem,
         scratch_shapes=[
+            pltpu.VMEM(qkv.shape, BF16),
             pltpu.VMEM(w_out.shape, BF16),
             pltpu.VMEM((2, half, width), BF16),
-            dma((2,)),
+            dma((3,)),
             pltpu.VMEM((3, half, width), F32),
             pltpu.VMEM((half, width), F32),
             pltpu.VMEM((half, width), F32),
@@ -529,6 +532,7 @@
 
 LIMIT = 16
 GROUP = 8
+DEPTH = 4
 
 
 def pick_kernel(want_ref, column_ref, table_ref, out_ref, fetched, sems):
@@ -554,13 +558,14 @@
     @pl.when(j == 0)
     def _():
         fetched[...] = jnp.zeros_like(fetched)
-        each(0, 0, lambda copy: copy.start())
-
-    @pl.when(j + 1 < pl.num_programs(0))
+        for ahead in range(DEPTH - 1):
+            each(ahead, ahead, lambda copy: copy.start())
+
+    @pl.when(j + DEPTH - 1 < pl.num_programs(0))
     def _():
-        each(j + 1, lax.rem(j + 1, 2), lambda copy: copy.start())
-
-    slot = lax.rem(j, 2)
+        each(j + DEPTH - 1, lax.rem(j + DEPTH - 1, DEPTH), lambda copy: copy.start())
+
+    slot = lax.rem(j, DEPTH)
     columns = lax.broadcasted_iota(jnp.int32, (LIMIT, LIMIT * GROUP), 1)
     place = lax.broadcasted_iota(jnp.int32, (LIMIT, LIMIT * GROUP), 0) * GROUP
     row = column_ref[...]
@@ -581,7 +586,7 @@
             pl.BlockSpec(memory_space=pl.ANY),
         ],
         out_specs=pl.BlockSpec((LIMIT, width), lambda j: (j, 0)),
-        scratch_shapes=[pltpu.VMEM((2, LIMIT, GROUP, width), BF16), pltpu.SemaphoreType.DMA((2, LIMIT))],
+        scratch_shapes=[pltpu.VMEM((DEPTH, LIMIT, GROUP, width), BF16), pltpu.SemaphoreType.DMA((DEPTH, LIMIT))],
         compiler_params=pltpu.CompilerParams(vmem_limit_bytes=VMEM_LIMIT),
         name="pick_rows",
     )(want, want.reshape(n * LIMIT, 1), table)

time: 510 us -> 510 us (level)
  no operation moved by 1% of the time
where the time goes in v4:
time: 510 us; the launch traced here: 508 us
  Pallas kernels  490 us (96%)
  other arithmetic  11.1 us (2%)
  local copies, waits for them, and re-layouts  6.12 us (1%)
    pallas_call x1, Pallas kernels, ring_out(): pl.pallas_call(functools.partial(ring_out_kernel, n, slots), out_shape=ja...  257 us
    pallas_call x1, Pallas kernels, ring_qkv(): pl.pallas_call(functools.partial(ring_qkv_kernel, n, pack), out_shape=jax...  136 us
    pallas_call x1, Pallas kernels, exchange(): pl.pallas_call(functools.partial(exchange_kernel, n), out_shape=jax.Shape...  82.1 us
    pallas_call x1, Pallas kernels, pick_rows(): pl.pallas_call(pick_kernel, grid=(n,), out_shape=jax.ShapeDtypeStruct((n...  14.6 us

profile of v4, /device:TPU:21, one launch (start us, length us, event | category | flops | bytes accessed | tf_op | source)
XLA Modules:
  0.0 508.5 jit_solution(2136072701486608317)
XLA Ops:
  0.7 1.4 convert_reduce_fusion.2
  2.1 0.7 broadcast_divide_fusion
  2.8 0.6 convert_reduce_fusion.1
  3.5 0.6 select_reduce_fusion.2
  4.8 101.8 %conditional.2 = (bf16[128,6144]{1,0:T(8,128)(2,1)}) conditional(s32[]{:T(128)} %convert_element_type.32, (s32[16,128]{1,0:T(8,128)S(1)}, s32[16,16,128]{2,1,0:T(8,128)S(1)}, s32[16,128]{1,0:T(8,128)S(1)}, s32[1,2048]{1,0:T(1,128)}, s32[]{:T(128)}, /*index=5*/bf16[3152,6144]{1,0:T(8,128)(2,1)}, s32[16,128]{1,0:T(8,128)}, ...), branch_computations={%region_3.0_spmd, %region_6.7_spmd} | conditional | flops 209284 | bytes 201286
  4.8 0.7 fusion.4
  5.5 0.2 select_reduce_fusion.1
  5.7 0.8 copy.16.index_ref
  6.4 0.7 subtract_add_fusion
  7.1 0.8 compare_reduce_fusion
  7.9 0.4 select_reduce_fusion
  8.3 0.8 sub.43.column_ref
  9.0 0.7 sub.33.want_ref
  9.7 14.6 %pick_rows.4 = bf16[256,6144]{1,0:T(8,128)(2,1)} custom-call(s32[256]{0:T(256)} %sub.33.want_ref, s32[256,1]{1,0:T(8,128)} %sub.43.column_ref, bf16[3152,6144]{1,0:T(8,128)(2,1)} %get-tuple-element.250.table_ref), custom_call_target="tpu_custom_call" | custom-call | tf_op jit(solution)/shard_map/cond/branch_0_fun/pick_rows/pallas_call | solution.py:579
  24.3 82.1 %exchange.4 = bf16[128,6144]{1,0:T(8,128)(2,1)} custom-call(bf16[16,16,6144]{2,1,0:T(8,128)(2,1)} %bitcast.32, s32[128,1]{1,0:T(8,128)} %copy.16.index_ref), custom_call_target="tpu_custom_call" | custom-call | tf_op jit(solution)/shard_map/cond/branch_0_fun/exchange/pallas_call | solution.py:645
  106.6 0.0 copy-start.1
  106.6 0.0 copy-start.2
  106.6 2.6 convert_reduce_fusion
  109.2 0.0 copy-start
  109.2 0.0 copy-start.3
  109.2 0.6 fusion.7
  109.8 0.5 copy-done
  110.4 0.0 copy-done.1
  110.4 0.0 copy-done.2
  110.4 1.8 fusion.10
  112.2 0.0 copy-done.3
  112.2 0.7 reshape.141.bias_ref
  112.9 135.9 %ring_qkv.1 = bf16[12,16,2,64,128]{4,3,2,1,0:T(8,128)(2,1)} custom-call(bf16[2,64,6144]{2,1,0:T(8,128)(2,1)} %bitcast.34, bf16[6,192,6144]{2,1,0:T(8,128)(2,1)} %bitcast.31, f32[6,1,192]{2,1,0:T(1,128)} %reshape.141.bias_ref), custom_call_target="tpu_custom_call" | custom-call | tf_op jit(solution)/shard_map/ring_qkv/pallas_call | solution.py:342
  248.8 257.0 %ring_out.1 = bf16[2,64,6144]{2,1,0:T(8,128)(2,1)} custom-call(bf16[12,2048,128]{2,1,0:T(8,128)(2,1)} %bitcast.30, bf16[4,96,6144]{2,1,0:T(8,128)(2,1)} %w_hbm.1, bf16[2,64,6144]{2,1,0:T(8,128)(2,1)} %bitcast.28, f32[1,6144]{1,0:T(1,128)} %bitcast.42), custom_call_target="tpu_custom_call" | custom-call | tf_op jit(solution)/shard_map/ring_out/pallas_call | solution.py:510
  505.8 2.7 copy.21
  (9 shorter events, 0.1 us)
Async XLA Ops:
  106.6 3.8 copy-start.1
  106.6 3.8 copy-start.2
  109.2 1.1 copy-start
  109.2 3.0 copy-start.3
